TPU v7x, 32 devices: a whole 2x2x4 slice. The times are simulated.
32 devices in a mesh: batch: 16 (over z, y, core), gene: 2 (over x).
Axes of the slice: x: 2, y: 2, z: 4, core: 2. Of those that a mesh axis runs over, the one named last changes fastest.
Arguments:
- umi_counts: int32 [16384, 8192], P('batch', 'gene'), may hold values from 0 to 65535
- cell_donors: int32 [16384], P('batch'), may hold values from 0 to 127
- cell_types: int32 [16384], P('batch'), may hold values from 0 to 23
- live_cells: int32 [16], P('batch'), may hold values from 1 to 1024, 10240 in all
- dosages: int32 [128, 2048], P(None, 'batch'), may hold values from 0 to 2
Outputs:
- scores: bfloat16 [24, 8192, 2048], P(None, ('gene', 'batch'))
All inputs are finite; a program needn't handle non-finite values. No bound on the sum of `live_cells` on one device may be relied on, other than what follows from the above.
Results may differ from a plain program's by a relative error of at most 0.0069.
Values may be sent and summed in bfloat16 or wider, within the bound.
A program may use at most 128 MiB of HBM per device.

v0:
```python
import jax
import jax.numpy as jnp
from jax import lax
from jax.sharding import PartitionSpec as P

TYPES = 24
DONORS = 128


def one_hot_rows(group_ids, total_groups):
    columns = jnp.arange(total_groups, dtype=jnp.int32)
    return (group_ids[:, None] == columns[None, :]).astype(jnp.bfloat16)


def standardize_dosage(block_dosage):
    genotype = block_dosage.astype(jnp.float32)
    centred = genotype - jnp.mean(genotype, axis=0, keepdims=True)
    return (centred * lax.rsqrt(jnp.mean(centred * centred, axis=0, keepdims=True) + 1e-06)).astype(
        jnp.bfloat16
    )


def on_device(umi_counts, cell_donors, cell_types, live_cells, dosages):
    total_groups = TYPES * DONORS
    cell_slots = umi_counts.shape[0]
    genes_block = umi_counts.shape[1]
    batch_count = lax.axis_size("batch")
    genes_local = genes_block // batch_count
    slot_index = jnp.arange(cell_slots, dtype=jnp.int32)
    alive_mask = slot_index < live_cells[0]
    cell_group = jnp.where(alive_mask, cell_types * DONORS + cell_donors, -1)
    rounded = umi_counts.astype(jnp.bfloat16)
    exchanged = lax.all_to_all(rounded, "batch", split_axis=1, concat_axis=0, tiled=True)
    all_groups = lax.all_gather(cell_group, "batch", axis=0, tiled=True)
    block_rows = 4 * cell_slots
    block_turns = batch_count // 4

    def add_block(step_index, totals):
        block_counts = lax.dynamic_slice_in_dim(exchanged, step_index * block_rows, block_rows, 0)
        block_groups = lax.dynamic_slice_in_dim(all_groups, step_index * block_rows, block_rows, 0)
        table = one_hot_rows(block_groups, total_groups)
        return totals + lax.dot_general(
            block_counts, table, (((0,), (0,)), ((), ())), preferred_element_type=jnp.float32
        )

    pseudo = lax.fori_loop(
        0, block_turns, add_block, jnp.zeros((genes_local, total_groups), jnp.float32)
    )
    partial_library = jnp.sum(pseudo, axis=0)
    library = jnp.maximum(lax.psum(partial_library, ("batch", "gene")), 1.0)
    logged = jnp.log1p(10000.0 * pseudo / library[None, :]).reshape(genes_local, TYPES, DONORS)
    centred = logged - jnp.mean(logged, axis=2, keepdims=True)
    standard = (
        centred * lax.rsqrt(jnp.mean(centred * centred, axis=2, keepdims=True) + 1e-06)
    ).astype(jnp.bfloat16)
    standard_rows = jnp.transpose(standard, (1, 0, 2)).reshape(TYPES * genes_local, DONORS)
    factor = DONORS ** (-0.5)
    geno_local = standardize_dosage(dosages)
    geno_piece = lax.all_gather(geno_local, "batch", axis=1, tiled=True)
    product = jnp.dot(standard_rows, geno_piece, preferred_element_type=jnp.float32) * factor
    return product.reshape(TYPES, genes_local, geno_piece.shape[1]).astype(jnp.bfloat16)


def solution(mesh):
    placed = (P("batch", "gene"), P("batch"), P("batch"), P("batch"), P(None, "batch"))
    return jax.shard_map(
        on_device,
        mesh=mesh,
        in_specs=placed,
        out_specs=P(None, ("gene", "batch"), None),
        check_vma=False,
    )
```

profile of v0, /device:TPU:14, one launch (start us, length us, event | category | flops | bytes accessed | tf_op | source)
XLA Modules:
  0.0 357.4 jit_solution(3607183109049914522)
XLA Ops:
  0.0 9.0 %convert_element_type.21 = bf16[1024,4096]{1,0:T(8,128)(2,1)} convert(s32[1024,4096]{1,0:T(8,128)} %param.7) | non-fusion elementwise | flops 4194304 | bytes 25165824 | tf_op jit(solution)/shard_map/convert_element_type | solution.py:32
  9.0 7.4 %copy.16 = bf16[128,16,8,256]{3,2,0,1:T(8,128)(2,1)} copy(bf16[128,16,8,256]{3,2,1,0:T(8,128)(2,1)} %bitcast.19) | data formatting | bytes 16777216 | tf_op jit(solution)/shard_map/all_to_all | solution.py:33
  16.5 0.0 copy-start.2
  16.5 0.0 copy-start.3
  16.5 0.0 copy-start.1
  16.5 6.4 %all-to-all-start = ((bf16[1024,16,256]{2,0,1:T(8,128)(2,1)}), bf16[1024,16,256]{2,0,1:T(8,128)(2,1)}, u32[]{:S(2)}, u32[]{:S(2)}) async-start(bf16[1024,16,256]{2,0,1:T(8,128)(2,1)} %bitcast.20), calls=%async_computation | async-start | bytes 16777216 | tf_op jit(solution)/shard_map/all_to_all | solution.py:33
  23.5 0.0 copy-done.2
  23.5 0.0 copy-done.3
  23.5 191.0 %all_gather.6 = s32[16384]{0:T(1024)S(1)} all-gather(s32[1024]{0:T(1024)S(1)} %add_select_fusion), channel_id=1, replica_groups=mesh['batch'=16,'gene'=2] {'batch'}, dimensions={0}, use_global_device_ids=true | all-gather | bytes 69632 | tf_op jit(solution)/shard_map/all_gather | solution.py:34
  214.5 0.0 copy-done.1
  214.6 18.3 %all_gather.7 = bf16[128,2048]{1,0:T(8,128)(2,1)} all-gather(bf16[128,128]{1,0:T(8,128)(2,1)S(1)} %multiply_convert_fusion.2), channel_id=1, replica_groups=mesh['batch'=16,'gene'=2] {'batch'}, dimensions={1}, use_global_device_ids=true | all-gather | bytes 557056 | tf_op jit(solution)/shard_map/all_gather | solution.py:59
  232.9 0.0 all-to-all-done
  232.9 57.8 %while.14 = (s32[]{:T(128)}, f32[256,3072]{1,0:T(8,128)S(1)}, bf16[16384,256]{1,0:T(8,128)(2,1)}, s32[16384]{0:T(1024)S(1)}, s32[]{:T(128)}, /*index=5*/s32[]{:T(128)}, s32[]{:T(128)}, s32[]{:T(128)}) while((s32[]{:T(128)}, f32[256,3072]{1,0:T(8,128)S(1)}, bf16[16384,256]{1,0:T(8,128)(2,1)}, s32[16384]{0:T(1024)S(1)}, s32[]{:T(128)}, ...), condition=%wide.region_1.2_spmd.clone, body=%wide.region_0.1_spmd.clone.sunk | while | flops 6456606720 | bytes 8437917 | solution.py:46
  232.9 14.4 %fusion.11 = f32[256,3072]{1,0:T(8,128)S(1)} fusion(s32[4096]{0:T(1024)S(1)} %dynamic_slice.21, f32[256,3072]{1,0:T(8,128)S(1)} %get-tuple-element.142, bf16[16384,256]{1,0:T(8,128)(2,1)} %get-tuple-element.151, s32[]{:T(128)S(6)} %select_n.16, pred[]{:T(512)S(6)} %compare.3), kind=kOutput, calls=%fused_computation.3.clone.1 | convolution fusion | flops 6456606720 | bytes 8404997 | tf_op jit(solution)/shard_map/while/body/eval_jaxpr/dot_general | solution.py:42
  247.4 14.4 %fusion.11 = f32[256,3072]{1,0:T(8,128)S(1)} fusion(s32[4096]{0:T(1024)S(1)} %dynamic_slice.21, f32[256,3072]{1,0:T(8,128)S(1)} %get-tuple-element.142, bf16[16384,256]{1,0:T(8,128)(2,1)} %get-tuple-element.151, s32[]{:T(128)S(6)} %select_n.16, pred[]{:T(512)S(6)} %compare.3), kind=kOutput, calls=%fused_computation.3.clone.1 | convolution fusion | flops 6456606720 | bytes 8404997 | tf_op jit(solution)/shard_map/while/body/eval_jaxpr/dot_general | solution.py:42
  261.8 14.4 %fusion.11 = f32[256,3072]{1,0:T(8,128)S(1)} fusion(s32[4096]{0:T(1024)S(1)} %dynamic_slice.21, f32[256,3072]{1,0:T(8,128)S(1)} %get-tuple-element.142, bf16[16384,256]{1,0:T(8,128)(2,1)} %get-tuple-element.151, s32[]{:T(128)S(6)} %select_n.16, pred[]{:T(512)S(6)} %compare.3), kind=kOutput, calls=%fused_computation.3.clone.1 | convolution fusion | flops 6456606720 | bytes 8404997 | tf_op jit(solution)/shard_map/while/body/eval_jaxpr/dot_general | solution.py:42
  276.3 14.4 %fusion.11 = f32[256,3072]{1,0:T(8,128)S(1)} fusion(s32[4096]{0:T(1024)S(1)} %dynamic_slice.21, f32[256,3072]{1,0:T(8,128)S(1)} %get-tuple-element.142, bf16[16384,256]{1,0:T(8,128)(2,1)} %get-tuple-element.151, s32[]{:T(128)S(6)} %select_n.16, pred[]{:T(512)S(6)} %compare.3), kind=kOutput, calls=%fused_computation.3.clone.1 | convolution fusion | flops 6456606720 | bytes 8404997 | tf_op jit(solution)/shard_map/while/body/eval_jaxpr/dot_general | solution.py:42
  290.7 2.5 copy.12
  293.3 0.2 reduce_sum.45
  293.4 44.2 %psum.7 = f32[3072]{0:T(1024)S(1)} all-reduce(f32[3072]{0:T(1024)S(1)} %reduce_sum.45), channel_id=1, replica_groups=mesh['batch'=16,'gene'=2] {'batch','gene'}, use_global_device_ids=true, to_apply=%region_3.4 | all-reduce | flops 3072 | bytes 24576 | tf_op jit(solution)/shard_map/psum | solution.py:50
  337.7 3.1 divide_log-plus-one_fusion
  340.8 0.2 reduce_sum.46
  341.1 0.4 multiply_reduce_fusion
  341.5 1.6 fusion.5
  343.1 0.0 copy-start
  343.1 2.0 copy.13
  345.0 0.0 copy-done
  345.0 12.4 %multiply_convert_fusion = bf16[6144,2048]{1,0:T(8,128)(2,1)} fusion(bf16[6144,128]{1,0:T(8,128)(2,1)S(1)} %bitcast.21, bf16[128,2048]{1,0:T(8,128)(2,1)S(1)} %copy-done), kind=kOutput, calls=%fused_computation.6 | convolution fusion | flops 3246391296 | bytes 27262976 | tf_op jit(solution)/shard_map/dot_general | solution.py:60
  (14 shorter events, 0.2 us)
Async XLA Ops:
  16.5 7.0 %copy-start.2 = (s32[1024]{0:T(1024)S(1)}, s32[1024]{0:T(1024)}, u32[]{:S(2)}) copy-start(s32[1024]{0:T(1024)} %param.8) | copy-start | bytes 12292
  16.5 7.0 %copy-start.3 = (s32[1024]{0:T(1024)S(1)}, s32[1024]{0:T(1024)}, u32[]{:S(2)}) copy-start(s32[1024]{0:T(1024)} %param.9) | copy-start | bytes 12292
  16.5 198.0 %copy-start.1 = (s32[128,128]{1,0:T(8,128)S(1)}, s32[128,128]{1,0:T(8,128)}, u32[]{:S(2)}) copy-start(s32[128,128]{1,0:T(8,128)} %param.11) | copy-start | bytes 196612
  16.5 216.4 %all-to-all-start = ((bf16[1024,16,256]{2,0,1:T(8,128)(2,1)}), bf16[1024,16,256]{2,0,1:T(8,128)(2,1)}, u32[]{:S(2)}, u32[]{:S(2)}) async-start(bf16[1024,16,256]{2,0,1:T(8,128)(2,1)} %bitcast.20), calls=%async_computation | async-start | bytes 16777216 | tf_op jit(solution)/shard_map/all_to_all | solution.py:33
  343.1 2.0 copy-start
where the time goes:
time: 358 us; the launch traced here: 357 us
  blocking collectives  253 us (71%)
  matrix products  70 us (20%)
  other arithmetic  14.7 us (4%)
  local copies, waits for them, and re-layouts  12 us (3%)
  starting transfers between devices  6.37 us (2%)
    all_gather x1, blocking collectives, on_device(): all_groups = lax.all_gather(cell_group, 'batch', axis=0, tiled=True)  191 us
    dot_general x4, matrix products, add_block(): lax.dot_general(block_counts, table, (((0,), (0,)), ((), ())), preferred_...  57.6 us
    psum x1, blocking collectives, on_device(): library = jnp.maximum(lax.psum(partial_library, ('batch', 'gene')), 1.0)  44.2 us
    all_gather x1, blocking collectives, on_device(): geno_piece = lax.all_gather(geno_local, 'batch', axis=1, tiled=True)  18.3 us
    dot_general x1, matrix products, on_device(): jnp.dot(standard_rows, geno_piece, preferred_element_type=jnp.float32)  12.4 us
    convert_element_type x1, other arithmetic, on_device(): rounded = umi_counts.astype(jnp.bfloat16)  9.05 us
    all_to_all x1, local copies, waits for them, and re-layouts, on_device(): lax.all_to_all(rounded, 'batch', split_axis=1, concat_axis=0, tiled=True)  7.43 us
  transfers between devices with their start and end apart: 1, of which 0 were waited for; matrix products, arithmetic and copies ran while one was open for 0% of the time, Pallas kernels for 0%

commit v1 on v0

--- a/solution.py
+++ b/solution.py
@@ -47,7 +47,7 @@
         0, block_turns, add_block, jnp.zeros((genes_local, total_groups), jnp.float32)
     )
     partial_library = jnp.sum(pseudo, axis=0)
-    library = jnp.maximum(lax.psum(partial_library, ("batch", "gene")), 1.0)
+    library = jnp.maximum(lax.psum(lax.psum(partial_library, "gene"), "batch"), 1.0)
     logged = jnp.log1p(10000.0 * pseudo / library[None, :]).reshape(genes_local, TYPES, DONORS)
     centred = logged - jnp.mean(logged, axis=2, keepdims=True)
     standard = (

time: 358 us -> 386 us (1.078)
  the two profiles are of different devices: /device:TPU:14 before, /device:TPU:0 now
where the time goes in v1:
time: 386 us; the launch traced here: 385 us
  blocking collectives  280 us (73%)
  matrix products  70 us (18%)
  other arithmetic  14.7 us (4%)
  local copies, waits for them, and re-layouts  12 us (3%)
  starting transfers between devices  7.6 us (2%)
    all_gather x1, blocking collectives, on_device(): all_groups = lax.all_gather(cell_group, 'batch', axis=0, tiled=True)  151 us
    all_gather x1, blocking collectives, on_device(): geno_piece = lax.all_gather(geno_local, 'batch', axis=1, tiled=True)  63.4 us
    dot_general x4, matrix products, add_block(): lax.dot_general(block_counts, table, (((0,), (0,)), ((), ())), preferred_...  57.6 us
    psum x1, blocking collectives, on_device(): lax.psum(lax.psum(partial_library, 'gene'), 'batch')  57.6 us
    dot_general x1, matrix products, on_device(): jnp.dot(standard_rows, geno_piece, preferred_element_type=jnp.float32)  12.4 us
    convert_element_type x1, other arithmetic, on_device(): rounded = umi_counts.astype(jnp.bfloat16)  9.05 us
    psum x1, blocking collectives, on_device(): lax.psum(partial_library, 'gene')  8.07 us
  transfers between devices with their start and end apart: 1, of which 0 were waited for; matrix products, arithmetic and copies ran while one was open for 0% of the time, Pallas kernels for 0%

profile of v1, /device:TPU:0, one launch (start us, length us, event | category | flops | bytes accessed | tf_op | source)
XLA Modules:
  0.0 385.5 jit_solution(17358757050728967967)
XLA Ops:
  0.0 9.0 %convert_element_type.21 = bf16[1024,4096]{1,0:T(8,128)(2,1)} convert(s32[1024,4096]{1,0:T(8,128)} %param.7) | non-fusion elementwise | flops 4194304 | bytes 25165824 | tf_op jit(solution)/shard_map/convert_element_type | solution.py:32
  9.0 7.4 %copy.16 = bf16[128,16,8,256]{3,2,0,1:T(8,128)(2,1)} copy(bf16[128,16,8,256]{3,2,1,0:T(8,128)(2,1)} %bitcast.19) | data formatting | bytes 16777216 | tf_op jit(solution)/shard_map/all_to_all | solution.py:33
  16.5 0.0 copy-start.2
  16.5 0.0 copy-start.3
  16.5 0.0 copy-start.1
  16.5 7.6 %all-to-all-start = ((bf16[1024,16,256]{2,0,1:T(8,128)(2,1)}), bf16[1024,16,256]{2,0,1:T(8,128)(2,1)}, u32[]{:S(2)}, u32[]{:S(2)}) async-start(bf16[1024,16,256]{2,0,1:T(8,128)(2,1)} %bitcast.20), calls=%async_computation | async-start | bytes 16777216 | tf_op jit(solution)/shard_map/all_to_all | solution.py:33
  24.7 0.0 copy-done.2
  24.8 0.0 copy-done.3
  24.8 151.2 %all_gather.6 = s32[16384]{0:T(1024)S(1)} all-gather(s32[1024]{0:T(1024)S(1)} %add_select_fusion), channel_id=1, replica_groups=mesh['batch'=16,'gene'=2] {'batch'}, dimensions={0}, use_global_device_ids=true | all-gather | bytes 69632 | tf_op jit(solution)/shard_map/all_gather | solution.py:34
  176.0 0.0 copy-done.1
  176.1 63.4 %all_gather.7 = bf16[128,2048]{1,0:T(8,128)(2,1)} all-gather(bf16[128,128]{1,0:T(8,128)(2,1)S(1)} %multiply_convert_fusion.2), channel_id=1, replica_groups=mesh['batch'=16,'gene'=2] {'batch'}, dimensions={1}, use_global_device_ids=true | all-gather | bytes 557056 | tf_op jit(solution)/shard_map/all_gather | solution.py:59
  239.6 0.0 all-to-all-done
  239.6 57.8 %while.14 = (s32[]{:T(128)}, f32[256,3072]{1,0:T(8,128)S(1)}, bf16[16384,256]{1,0:T(8,128)(2,1)}, s32[16384]{0:T(1024)S(1)}, s32[]{:T(128)}, /*index=5*/s32[]{:T(128)}, s32[]{:T(128)}, s32[]{:T(128)}) while((s32[]{:T(128)}, f32[256,3072]{1,0:T(8,128)S(1)}, bf16[16384,256]{1,0:T(8,128)(2,1)}, s32[16384]{0:T(1024)S(1)}, s32[]{:T(128)}, ...), condition=%wide.region_1.2_spmd.clone, body=%wide.region_0.1_spmd.clone.sunk | while | flops 6456606720 | bytes 8437917 | solution.py:46
  239.6 14.4 %fusion.11 = f32[256,3072]{1,0:T(8,128)S(1)} fusion(s32[4096]{0:T(1024)S(1)} %dynamic_slice.21, f32[256,3072]{1,0:T(8,128)S(1)} %get-tuple-element.142, bf16[16384,256]{1,0:T(8,128)(2,1)} %get-tuple-element.151, s32[]{:T(128)S(6)} %select_n.16, pred[]{:T(512)S(6)} %compare.3), kind=kOutput, calls=%fused_computation.3.clone.1 | convolution fusion | flops 6456606720 | bytes 8404997 | tf_op jit(solution)/shard_map/while/body/eval_jaxpr/dot_general | solution.py:42
  254.0 14.4 %fusion.11 = f32[256,3072]{1,0:T(8,128)S(1)} fusion(s32[4096]{0:T(1024)S(1)} %dynamic_slice.21, f32[256,3072]{1,0:T(8,128)S(1)} %get-tuple-element.142, bf16[16384,256]{1,0:T(8,128)(2,1)} %get-tuple-element.151, s32[]{:T(128)S(6)} %select_n.16, pred[]{:T(512)S(6)} %compare.3), kind=kOutput, calls=%fused_computation.3.clone.1 | convolution fusion | flops 6456606720 | bytes 8404997 | tf_op jit(solution)/shard_map/while/body/eval_jaxpr/dot_general | solution.py:42
  268.5 14.4 %fusion.11 = f32[256,3072]{1,0:T(8,128)S(1)} fusion(s32[4096]{0:T(1024)S(1)} %dynamic_slice.21, f32[256,3072]{1,0:T(8,128)S(1)} %get-tuple-element.142, bf16[16384,256]{1,0:T(8,128)(2,1)} %get-tuple-element.151, s32[]{:T(128)S(6)} %select_n.16, pred[]{:T(512)S(6)} %compare.3), kind=kOutput, calls=%fused_computation.3.clone.1 | convolution fusion | flops 6456606720 | bytes 8404997 | tf_op jit(solution)/shard_map/while/body/eval_jaxpr/dot_general | solution.py:42
  282.9 14.4 %fusion.11 = f32[256,3072]{1,0:T(8,128)S(1)} fusion(s32[4096]{0:T(1024)S(1)} %dynamic_slice.21, f32[256,3072]{1,0:T(8,128)S(1)} %get-tuple-element.142, bf16[16384,256]{1,0:T(8,128)(2,1)} %get-tuple-element.151, s32[]{:T(128)S(6)} %select_n.16, pred[]{:T(512)S(6)} %compare.3), kind=kOutput, calls=%fused_computation.3.clone.1 | convolution fusion | flops 6456606720 | bytes 8404997 | tf_op jit(solution)/shard_map/while/body/eval_jaxpr/dot_general | solution.py:42
  297.4 2.5 copy.12
  299.9 0.2 reduce_sum.45
  300.1 8.1 %psum.14 = f32[3072]{0:T(1024)S(1)} all-reduce(f32[3072]{0:T(1024)S(1)} %reduce_sum.45), channel_id=1, replica_groups=mesh['batch'=16,'gene'=2] {'gene'}, use_global_device_ids=true, to_apply=%region_3.4 | all-reduce | flops 3072 | bytes 24576 | tf_op jit(solution)/shard_map/psum | solution.py:50
  308.1 57.6 %psum.15 = f32[3072]{0:T(1024)S(1)} all-reduce(f32[3072]{0:T(1024)S(1)} %psum.14), channel_id=1, replica_groups=mesh['batch'=16,'gene'=2] {'batch'}, use_global_device_ids=true, to_apply=%region_4.5 | all-reduce | flops 3072 | bytes 24576 | tf_op jit(solution)/shard_map/psum | solution.py:50
  365.8 3.1 divide_log-plus-one_fusion
  368.9 0.2 reduce_sum.46
  369.1 0.4 multiply_reduce_fusion
  369.6 1.6 fusion.5
  371.1 0.0 copy-start
  371.2 2.0 copy.13
  373.1 0.0 copy-done
  373.1 12.4 %multiply_convert_fusion = bf16[6144,2048]{1,0:T(8,128)(2,1)} fusion(bf16[6144,128]{1,0:T(8,128)(2,1)S(1)} %bitcast.21, bf16[128,2048]{1,0:T(8,128)(2,1)S(1)} %copy-done), kind=kOutput, calls=%fused_computation.6 | convolution fusion | flops 3246391296 | bytes 27262976 | tf_op jit(solution)/shard_map/dot_general | solution.py:60
  (14 shorter events, 0.2 us)
Async XLA Ops:
  16.5 8.3 %copy-start.2 = (s32[1024]{0:T(1024)S(1)}, s32[1024]{0:T(1024)}, u32[]{:S(2)}) copy-start(s32[1024]{0:T(1024)} %param.8) | copy-start | bytes 12292
  16.5 8.3 %copy-start.3 = (s32[1024]{0:T(1024)S(1)}, s32[1024]{0:T(1024)}, u32[]{:S(2)}) copy-start(s32[1024]{0:T(1024)} %param.9) | copy-start | bytes 12292
  16.5 159.5 %copy-start.1 = (s32[128,128]{1,0:T(8,128)S(1)}, s32[128,128]{1,0:T(8,128)}, u32[]{:S(2)}) copy-start(s32[128,128]{1,0:T(8,128)} %param.11) | copy-start | bytes 196612
  16.5 223.1 %all-to-all-start = ((bf16[1024,16,256]{2,0,1:T(8,128)(2,1)}), bf16[1024,16,256]{2,0,1:T(8,128)(2,1)}, u32[]{:S(2)}, u32[]{:S(2)}) async-start(bf16[1024,16,256]{2,0,1:T(8,128)(2,1)} %bitcast.20), calls=%async_computation | async-start | bytes 16777216 | tf_op jit(solution)/shard_map/all_to_all | solution.py:33
  371.1 2.0 copy-start
